TPU v7x, 32 devices: a whole 2x2x4 slice. The times are simulated.
32 devices in a mesh: rows: 16 (over z, x, core), cols: 2 (over y).
Axes of the slice: x: 2, y: 2, z: 4, core: 2. Of those that a mesh axis runs over, the one named last changes fastest.
Arguments:
- current_frame: bfloat16 [128, 256, 256], P(None, 'rows', 'cols'), may hold values from -6 to 6
- history_frames: bfloat16 [3, 128, 256, 256], P(None, None, 'rows', 'cols'), may hold values from -6 to 6
- offsets: int32 [3, 2], replicated, may hold values from -16 to 16, as said below
- compress_weight: bfloat16 [32, 128], replicated, may hold values from -0.5 to 0.5
- mixer_weight: bfloat16 [3, 3, 128, 224], replicated, may hold values from -0.125 to 0.125
- mixer_bias: float32 [128], replicated, may hold values from -3 to 3
Outputs:
- joined_grid: bfloat16 [128, 256, 256], P(None, 'rows', 'cols')
Inputs may be any that keep to these rules, and one draw needn't show every extreme that they name: offsets[k, 0] lies in -8..8 and offsets[k, 1] in -16..16; no offset is 0; in each of the two columns one frame's offset equals the bound and another equals its negative.
All inputs are finite; a program needn't handle non-finite values.
Results may differ from a plain program's by a relative error of at most 0.0034.
Values may be sent and summed in bfloat16 or wider, within the bound.
A program may use at most 64 MiB of HBM per device.

v0:
```python
import jax
import jax.numpy as jnp
from jax import lax
from jax.sharding import PartitionSpec as P

CP = 32
SHIFT_X = 16


def with_halo(shard, sides, width):
    for axis, dim in sides:
        size, length = (lax.axis_size(axis), shard.shape[dim])
        up = [(i, (i + 1) % size) for i in range(size - 1)]
        down = [(j, i) for i, j in up]
        last = lax.slice_in_dim(shard, length - width, length, axis=dim)
        first = lax.slice_in_dim(shard, 0, width, axis=dim)
        before = lax.ppermute(last, axis, up)
        after = lax.ppermute(first, axis, down)
        shard = jnp.concatenate([before, shard, after], axis=dim)
    return shard


def conv_taps(present_rows, older_rows, mixer_weight, mixer_bias):
    height = present_rows.shape[1] - 2
    width = present_rows.shape[2] - 2
    channels = present_rows.shape[0]
    total = jnp.zeros((mixer_weight.shape[2], height * width), jnp.float32)
    for tap_row in range(3):
        for tap_col in range(3):
            present = present_rows[
                :, tap_row : tap_row + height, tap_col : tap_col + width
            ].reshape(channels, -1)
            older = older_rows[:, tap_row : tap_row + height, tap_col : tap_col + width].reshape(
                older_rows.shape[0], -1
            )
            total = total + jnp.dot(
                mixer_weight[tap_row, tap_col, :, :channels],
                present,
                preferred_element_type=jnp.float32,
            )
            total = total + jnp.dot(
                mixer_weight[tap_row, tap_col, :, channels:],
                older,
                preferred_element_type=jnp.float32,
            )
    result = jnp.maximum(total + mixer_bias[:, None], 0.0)
    return result.astype(jnp.bfloat16).reshape(-1, height, width)


def pack_block(values, depth, extent, breadth):
    flat_values = values.reshape(-1)
    padding = depth * extent * breadth - flat_values.shape[0]
    flat_values = jnp.concatenate([flat_values, jnp.zeros((padding,), flat_values.dtype)])
    return flat_values.reshape(depth, extent, breadth)


def body(current_frame, history_frames, offsets, compress_weight, mixer_weight, mixer_bias):
    frames, channels, local_rows, local_cols = history_frames.shape
    reach_rows = local_rows // 2 + 1
    reach_cols = SHIFT_X + 1
    row_half = min(reach_rows, local_rows // 2)
    row_depth = -(-channels // row_half)
    reduced = jnp.einsum(
        "oc,fcrx->forx", compress_weight, history_frames, preferred_element_type=jnp.float32
    ).astype(jnp.bfloat16)
    source = reduced.reshape(frames * CP, local_rows, local_cols)
    channel_depth = CP
    first_piece = pack_block(current_frame[:, 0, :], row_depth, row_half, local_cols)
    last_piece = pack_block(current_frame[:, local_rows - 1, :], row_depth, row_half, local_cols)
    middle = jnp.zeros((row_depth, local_rows - 2 * row_half, local_cols), jnp.bfloat16)
    edge_slab = jnp.concatenate([first_piece, middle, last_piece], axis=1)
    source = jnp.concatenate([source, edge_slab], axis=0)
    source = with_halo(source, (("rows", 1),), reach_rows)
    carried = source[source.shape[0] - row_depth :]
    source = source[: source.shape[0] - row_depth]
    above_row = carried[:, reach_rows - row_half : reach_rows, :].reshape(-1, local_cols)
    below_row = carried[:, reach_rows + local_rows : reach_rows + local_rows + row_half, :].reshape(
        -1, local_cols
    )
    present_middle = jnp.concatenate(
        [above_row[:, None, :], current_frame, below_row[:, None, :]], axis=1
    )
    row_span = source.shape[1]
    col_half = min(reach_cols, local_cols // 2)
    edge_count = channels * (local_rows + 2)
    col_depth = -(-edge_count // (row_span * col_half))
    first_piece = pack_block(present_middle[:, :, 0], col_depth, row_span, col_half)
    last_piece = pack_block(present_middle[:, :, local_cols - 1], col_depth, row_span, col_half)
    middle = jnp.zeros((col_depth, row_span, local_cols - 2 * col_half), jnp.bfloat16)
    edge_slab = jnp.concatenate([first_piece, middle, last_piece], axis=2)
    source = jnp.concatenate([source, edge_slab], axis=0)
    source = with_halo(source, (("cols", 2),), reach_cols)
    carried = source[source.shape[0] - col_depth :]
    source = source[: source.shape[0] - col_depth]
    left_col = (
        carried[:, :, reach_cols - col_half : reach_cols]
        .reshape(-1)[:edge_count]
        .reshape(channels, local_rows + 2)
    )
    right_col = (
        carried[:, :, reach_cols + local_cols : reach_cols + local_cols + col_half]
        .reshape(-1)[:edge_count]
        .reshape(channels, local_rows + 2)
    )
    present_rows = jnp.concatenate(
        [left_col[:, :, None], present_middle, right_col[:, :, None]], axis=2
    )
    pieces = []
    for frame_index in range(frames):
        start_row = reach_rows - 1 - offsets[frame_index, 0]
        start_col = reach_cols - 1 - offsets[frame_index, 1]
        window = lax.dynamic_slice(
            source,
            (jnp.int32(frame_index * channel_depth), start_row, start_col),
            (channel_depth, local_rows + 2, local_cols + 2),
        )
        pieces.append(window)
    shifted = jnp.concatenate(pieces, axis=0)
    row_places = (
        lax.axis_index("rows") * local_rows - 1 + jnp.arange(local_rows + 2, dtype=jnp.int32)
    )
    col_places = (
        lax.axis_index("cols") * local_cols - 1 + jnp.arange(local_cols + 2, dtype=jnp.int32)
    )
    row_inside = (row_places >= 0) & (row_places < local_rows * lax.axis_size("rows"))
    col_inside = (col_places >= 0) & (col_places < local_cols * lax.axis_size("cols"))
    inside = row_inside[:, None] & col_inside[None, :]
    shifted = jnp.where(inside[None, :, :], shifted, jnp.zeros_like(shifted))
    return conv_taps(present_rows, shifted, mixer_weight, mixer_bias)


def solution(mesh):
    in_specs = (P(None, "rows", "cols"), P(None, None, "rows", "cols"), P(), P(), P(), P())
    out_specs = P(None, "rows", "cols")
    return jax.shard_map(body, mesh=mesh, in_specs=in_specs, out_specs=out_specs, check_vma=False)
```

profile of v0, /device:TPU:8, one launch (start us, length us, event | category | flops | bytes accessed | tf_op | source)
XLA Modules:
  0.0 75.1 jit_solution(5194914580803888980)
XLA Ops:
  0.0 1.3 %fusion.87 = (bf16[128,1,128]{2,1,0:T(2,128)(2,1)S(1)}, bf16[128,1,128]{2,1,0:T(2,128)(2,1)S(1)}) fusion(bf16[128,16,128]{2,1,0:T(8,128)(2,1)} %param.6), kind=kLoop, calls=%fused_computation.129 | loop fusion | bytes 131072 | tf_op jit(solution)/shard_map/slice | solution.py:68
  1.6 1.1 %fusion.18 = bf16[3,32,16,128]{3,1,2,0:T(8,128)(2,1)S(1)} fusion(bf16[3,128,16,128]{3,2,1,0:T(8,128)(2,1)S(1)} %copy-done, bf16[32,128]{1,0:T(8,128)(2,1)} %param.9), kind=kOutput, calls=%fused_computation.38 | convolution fusion | flops 50528256 | bytes 1974272 | tf_op jit(solution)/shard_map/oc,fcrx->forx/dot_general | solution.py:63
  2.9 1.1 %fusion.88 = (bf16[112,9,128]{2,1,0:T(8,128)(2,1)}, bf16[112,9,128]{2,1,0:T(8,128)(2,1)}) fusion(bf16[112,16,128]{2,1,0:T(8,128)(2,1)S(1)} %maximum_maximum_fusion.2), kind=kLoop, calls=%fused_computation.130 | loop fusion | bytes 1032192 | tf_op jit(solution)/shard_map/slice | solution.py:15
  4.0 1.9 %collective-permute-start = (bf16[112,9,128]{2,1,0:T(8,128)(2,1)}, bf16[112,9,128]{2,1,0:T(8,128)(2,1)S(1)}, u32[]{:S(2)}, u32[]{:S(2)}) collective-permute-start(bf16[112,9,128]{2,1,0:T(8,128)(2,1)} %get-tuple-element.33), channel_id=1, source_target_pairs={{0,2},{2,4},{4,6},{6,8},{8,10},{10,12},{12,14},{14,16},{16,18},{18... | collective-permute-start | bytes 774152 | tf_op jit(solution)/shard_map/ppermute | solution.py:17
  6.0 4.5 %collective-permute-start.1 = (bf16[112,9,128]{2,1,0:T(8,128)(2,1)}, bf16[112,9,128]{2,1,0:T(8,128)(2,1)}, u32[]{:S(2)}, u32[]{:S(2)}) collective-permute-start(bf16[112,9,128]{2,1,0:T(8,128)(2,1)} %get-tuple-element.34), channel_id=1, source_target_pairs={{2,0},{4,2},{6,4},{8,6},{10,8},{12,10},{14,12},{16,14},{18,16},{20... | collective-permute-start | bytes 774152 | tf_op jit(solution)/shard_map/ppermute | solution.py:18
  10.5 0.7 broadcast_and_fusion
  11.2 0.7 fusion.89
  11.9 0.5 copy.27
  20.1 0.7 copy.37
  20.8 1.4 %slice_bitcast_fusion = bf16[128,1,128]{2,0,1:T(8,128)(2,1)} fusion(bf16[112,9,128]{2,1,0:T(8,128)(2,1)} %collective-permute-done.1), kind=kLoop, calls=%fused_computation.74 | loop fusion | bytes 65536 | tf_op jit(solution)/shard_map/broadcast_in_dim;reshape | solution.py:81
  22.2 0.9 %copy.28 = bf16[128,1,128]{0,2,1:T(8,128)(2,1)S(1)} copy(bf16[128,1,128]{2,0,1:T(8,128)(2,1)} %slice_bitcast_fusion) | data formatting | bytes 65536 | tf_op jit(solution)/shard_map/broadcast_in_dim;reshape | solution.py:81
  23.0 1.4 %copy.41 = bf16[128,1,128]{2,1,0:T(2,128)(2,1)} copy(bf16[128,1,128]{2,0,1:T(8,128)(2,1)} %slice_bitcast_fusion) | data formatting | bytes 65536 | tf_op jit(solution)/shard_map/broadcast_in_dim;reshape | solution.py:81
  24.5 0.6 pad_maximum_fusion.14
  25.1 0.7 copy.29
  25.8 0.9 %reshape_squeeze.6 = bf16[2304]{0:T(1024)(128)(2,1)S(1)} reshape(bf16[128,18,1]{1,0,2:T(8,128)(2,1)} %copy.29) | data formatting | bytes 9216 | tf_op jit(solution)/shard_map/reshape;squeeze | solution.py:51
  27.0 0.8 %copy.30 = bf16[128,18,1]{1,0,2:T(8,128)(2,1)S(1)} copy(bf16[128,18,1]{0,2,1:T(2,128)(2,1)} %get-tuple-element.28) | data formatting | bytes 9216 | tf_op jit(solution)/shard_map/slice | solution.py:88
  28.0 0.6 concatenate.52
  28.6 0.9 %reshape.140 = bf16[4,34,17]{2,1,0:T(8,128)(2,1)S(1)} reshape(bf16[2312]{0:T(1024)(128)(2,1)} %concatenate.52) | data formatting | bytes 9248 | tf_op jit(solution)/shard_map/reshape | solution.py:54
  29.5 1.5 %pad_maximum_fusion.5 = bf16[96,34,128]{2,1,0:T(8,128)(2,1)S(1)} fusion(bf16[112,9,128]{2,1,0:T(8,128)(2,1)} %collective-permute-done.1, bf16[112,9,128]{2,1,0:T(8,128)(2,1)} %copy-done.16, bf16[96,16,128]{2,1,0:T(8,128)(2,1)S(1)} %bitcast.195, bf16[16,8,128]{2,1,0:T(8,128)(2,1)} %copy-done.22, bf16[16,8,128]{2,1,0:T(8,128)(2,1)} %copy-done.23), kind=kLoop, calls=%fused_computation.41 | loop fusion | flops 4177920 | bytes 1810432 | tf_op jit(solution)/shard_map/concatenate | solution.py:19
  31.2 1.7 %fusion.84 = (bf16[100,34,17]{2,1,0:T(8,128)(2,1)}, bf16[100,34,17]{2,1,0:T(8,128)(2,1)}) fusion(bf16[100,34,128]{2,1,0:T(8,128)(2,1)S(1)} %maximum_maximum_fusion), kind=kLoop, calls=%fused_computation.126 | loop fusion | bytes 462400 | tf_op jit(solution)/shard_map/slice | solution.py:16
  32.9 2.5 %copy.31 = bf16[100,34,17]{0,1,2:T(8,128)(2,1)} copy(bf16[100,34,17]{2,1,0:T(8,128)(2,1)} %get-tuple-element.18) | data formatting | bytes 231200 | tf_op jit(solution)/shard_map/slice | solution.py:15
  35.4 3.4 %collective-permute-start.2 = (bf16[100,34,17]{0,1,2:T(8,128)(2,1)}, bf16[100,34,17]{0,1,2:T(8,128)(2,1)S(1)}, u32[]{:S(2)}, u32[]{:S(2)}) collective-permute-start(bf16[100,34,17]{0,1,2:T(8,128)(2,1)} %copy.31), channel_id=1, source_target_pairs={{0,1},{2,3},{4,5},{6,7},{8,9},{10,11},{12,13},{14,15},{16,17},{18,... | collective-permute-start | bytes 346808 | tf_op jit(solution)/shard_map/ppermute | solution.py:17
  38.8 2.5 %copy.34 = bf16[100,34,17]{0,1,2:T(8,128)(2,1)} copy(bf16[100,34,17]{2,1,0:T(8,128)(2,1)} %get-tuple-element.17) | data formatting | bytes 231200 | tf_op jit(solution)/shard_map/slice | solution.py:16
  41.3 1.3 %collective-permute-start.3 = (bf16[100,34,17]{0,1,2:T(8,128)(2,1)}, bf16[100,34,17]{0,1,2:T(8,128)(2,1)S(1)}, u32[]{:S(2)}, u32[]{:S(2)}) collective-permute-start(bf16[100,34,17]{0,1,2:T(8,128)(2,1)} %copy.34), channel_id=1, source_target_pairs={{1,0},{3,2},{5,4},{7,6},{9,8},{11,10},{13,12},{15,14},{17,16},{19,... | collective-permute-start | bytes 346808 | tf_op jit(solution)/shard_map/ppermute | solution.py:18
  42.5 2.4 %pad_maximum_fusion.10 = (bf16[128,16,128]{2,1,0:T(8,128)(2,1)}, bf16[128,16,128]{2,1,0:T(8,128)(2,1)}) fusion(bf16[128,1,128]{2,1,0:T(2,128)(2,1)} %copy.41, bf16[128,16,128]{2,1,0:T(8,128)(2,1)S(1)} %copy-done.1, bf16[128,1,128]{2,1,0:T(2,128)(2,1)} %copy.37), kind=kLoop, calls=%fused_computation.53 | loop fusion | flops 2097152 | bytes 1638400 | tf_op jit(solution)/shard_map/concatenate | solution.py:80
  44.9 1.6 %copy.35 = bf16[100,34,17]{2,1,0:T(8,128)(2,1)} copy(bf16[100,34,17]{0,1,2:T(8,128)(2,1)S(1)} %collective-permute-done.2) | data formatting | bytes 231200 | tf_op jit(solution)/shard_map/ppermute | solution.py:17
  46.5 2.3 %collective-permute-done.3 = bf16[100,34,17]{0,1,2:T(8,128)(2,1)S(1)} collective-permute-done((bf16[100,34,17]{0,1,2:T(8,128)(2,1)}, bf16[100,34,17]{0,1,2:T(8,128)(2,1)S(1)}, u32[]{:S(2)}, u32[]{:S(2)}) %collective-permute-start.3) | collective-permute-done | bytes 115632 | tf_op jit(solution)/shard_map/ppermute | solution.py:18
  48.8 1.6 %copy.36 = bf16[100,34,17]{2,1,0:T(8,128)(2,1)} copy(bf16[100,34,17]{0,1,2:T(8,128)(2,1)S(1)} %collective-permute-done.3) | data formatting | bytes 231200 | tf_op jit(solution)/shard_map/ppermute | solution.py:18
  50.3 3.6 %pad_maximum_fusion = bf16[96,34,162]{2,1,0:T(8,128)(2,1)S(1)} fusion(bf16[100,34,17]{2,1,0:T(8,128)(2,1)} %copy.36, bf16[100,34,17]{2,1,0:T(8,128)(2,1)} %copy.35, bf16[96,34,128]{2,1,0:T(8,128)(2,1)S(1)} %pad_maximum_fusion.5, bf16[4,34,17]{2,1,0:T(8,128)(2,1)S(1)} %reshape.140, bf16[4,34,94]{2,1,0:T(8,128)(2,1)S(1)} %broadcast_in_dim.18, ...), kind=kLoop, calls=%fused_computation.30 | loop fusion | flops 6345216 | bytes 2159136 | tf_op jit(solution)/shard_map/concatenate | solution.py:19
  54.0 0.8 %constant_dynamic-slice_fusion.2 = (bf16[32,18,130]{2,1,0:T(8,128)(2,1)S(1)}, bf16[32,18,130]{2,1,0:T(8,128)(2,1)S(1)}, bf16[32,18,130]{2,1,0:T(8,128)(2,1)S(1)}) fusion(bf16[96,34,162]{2,1,0:T(8,128)(2,1)S(1)} %pad_maximum_fusion, s32[]{:T(128)S(6)} %select_n.22, s32[]{:T(128)S(6)} %select_n.23, s32[]{:T(128)S(6)} %select_n.24, s32[]{:T(128)S(6)} %select_n.25, ...), kind=kLoop, calls=%fused_computation.124 | loop fusion | bytes 898584 | tf_op jit(solution)/shard_map/dynamic_slice | solution.py:112
  55.2 2.4 %fusion.83 = (bf16[96,16,128]{2,1,0:T(8,128)(2,1)}, bf16[96,16,128]{2,1,0:T(8,128)(2,1)S(1)}, bf16[96,16,128]{2,1,0:T(8,128)(2,1)S(1)}, bf16[96,16,128]{2,1,0:T(...) fusion(bf16[96,18,130]{2,1,0:T(8,128)(2,1)S(1)} %maximum_select, ...), kind=kLoop, calls=%fused_computation.125 | loop fusion | bytes 7077888 | tf_op jit(solution)/shard_map/slice | solution.py:33
  57.7 0.8 %slice.251 = bf16[4,34,17]{0,1,2:T(8,128)(2,1)} slice(bf16[100,34,17]{0,1,2:T(8,128)(2,1)S(1)} %copy-done.15), slice={[96:100], [0:34], [0:17]} | slice | bytes 9248 | tf_op jit(solution)/shard_map/slice | solution.py:96
  58.4 1.3 %copy.32 = bf16[4,34,17]{2,1,0:T(8,128)(2,1)S(1)} copy(bf16[4,34,17]{0,1,2:T(8,128)(2,1)} %slice.251) | data formatting | bytes 9248 | tf_op jit(solution)/shard_map/slice | solution.py:96
  60.2 1.7 %slice.257 = bf16[4,34,17]{0,1,2:T(8,128)(2,1)} slice(bf16[100,34,17]{0,1,2:T(8,128)(2,1)} %copy-done.13), slice={[96:100], [0:34], [0:17]} | slice | bytes 9248 | tf_op jit(solution)/shard_map/slice | solution.py:101
  61.9 1.3 %copy.38 = bf16[4,34,17]{2,1,0:T(8,128)(2,1)S(1)} copy(bf16[4,34,17]{0,1,2:T(8,128)(2,1)} %slice.257) | data formatting | bytes 9248 | tf_op jit(solution)/shard_map/slice | solution.py:101
  64.0 0.4 fusion.86
  64.7 0.7 copy-done.17
  66.1 0.4 copy-done.5
  67.5 0.4 copy-done.9
  68.5 0.4 copy-done.8
  69.2 0.3 convolution_add_fusion
  70.5 0.4 copy-done.6
  71.8 0.4 copy-done.4
  72.2 0.3 fusion.5
  72.6 0.3 fusion.4
  73.2 0.3 copy-done.12
  73.6 0.3 fusion.12
  73.9 1.2 %copy.42 = bf16[128,16,128]{2,1,0:T(8,128)(2,1)} copy(bf16[128,16,128]{0,2,1:T(8,128)(2,1)S(1)} %bitcast.196) | data formatting | bytes 1048576 | tf_op jit(solution)/shard_map/reshape | solution.py:47
  (85 shorter events, 7.7 us)
Async XLA Ops:
  0.0 1.6 %copy-start = (bf16[3,128,16,128]{3,2,1,0:T(8,128)(2,1)S(1)}, bf16[3,128,16,128]{3,2,1,0:T(8,128)(2,1)}, u32[]{:S(2)}) copy-start(bf16[3,128,16,128]{3,2,1,0:T(8,128)(2,1)} %param.7) | copy-start | bytes 4718596
  2.6 8.6 %copy-start.25 = (s32[3,2]{0,1:T(2,128)S(1)}, s32[3,2]{0,1:T(2,128)}, u32[]{:S(2)}) copy-start(s32[3,2]{0,1:T(2,128)} %param.8) | copy-start | bytes 76
  2.6 9.2 %copy-start.1 = (bf16[128,16,128]{2,1,0:T(8,128)(2,1)S(1)}, bf16[128,16,128]{2,1,0:T(8,128)(2,1)}, u32[]{:S(2)}) copy-start(bf16[128,16,128]{2,1,0:T(8,128)(2,1)} %param.6) | copy-start | bytes 1572868
  2.8 1.2 %copy-start.22 = (bf16[16,8,128]{2,1,0:T(8,128)(2,1)}, bf16[16,8,128]{2,1,0:T(8,128)(2,1)S(1)}, u32[]{:S(2)}) copy-start(bf16[16,8,128]{2,1,0:T(8,128)(2,1)S(1)} %get-tuple-element.41) | copy-start | bytes 98308
  2.8 1.2 %copy-start.23 = (bf16[16,8,128]{2,1,0:T(8,128)(2,1)}, bf16[16,8,128]{2,1,0:T(8,128)(2,1)S(1)}, u32[]{:S(2)}) copy-start(bf16[16,8,128]{2,1,0:T(8,128)(2,1)S(1)} %get-tuple-element.42) | copy-start | bytes 98308
  4.0 15.9 %collective-permute-start = (bf16[112,9,128]{2,1,0:T(8,128)(2,1)}, bf16[112,9,128]{2,1,0:T(8,128)(2,1)S(1)}, u32[]{:S(2)}, u32[]{:S(2)}) collective-permute-start(bf16[112,9,128]{2,1,0:T(8,128)(2,1)} %get-tuple-element.33), channel_id=1, source_target_pairs={{0,2},{2,4},{4,6},{6,8},{8,10},{10,12},{12,14},{14,16},{16,18},{18... | collective-permute-start | bytes 774152 | tf_op jit(solution)/shard_map/ppermute | solution.py:17
  6.0 14.8 %collective-permute-start.1 = (bf16[112,9,128]{2,1,0:T(8,128)(2,1)}, bf16[112,9,128]{2,1,0:T(8,128)(2,1)}, u32[]{:S(2)}, u32[]{:S(2)}) collective-permute-start(bf16[112,9,128]{2,1,0:T(8,128)(2,1)} %get-tuple-element.34), channel_id=1, source_target_pairs={{2,0},{4,2},{6,4},{8,6},{10,8},{12,10},{14,12},{16,14},{18,16},{20... | collective-permute-start | bytes 774152 | tf_op jit(solution)/shard_map/ppermute | solution.py:18
  12.3 16.2 %copy-start.2 = (bf16[128,16,128]{0,2,1:T(8,128)(2,1)}, bf16[128,16,128]{0,2,1:T(8,128)(2,1)S(1)}, u32[]{:S(2)}) copy-start(bf16[128,16,128]{0,2,1:T(8,128)(2,1)S(1)} %copy.27) | copy-start | bytes 1572868
  19.9 8.6 %copy-start.16 = (bf16[112,9,128]{2,1,0:T(8,128)(2,1)}, bf16[112,9,128]{2,1,0:T(8,128)(2,1)S(1)}, u32[]{:S(2)}) copy-start(bf16[112,9,128]{2,1,0:T(8,128)(2,1)S(1)} %collective-permute-done) | copy-start | bytes 774148
  20.1 6.7 %copy-start.18 = (bf16[128,1,128]{0,2,1:T(8,128)(2,1)}, bf16[128,1,128]{0,2,1:T(8,128)(2,1)S(1)}, u32[]{:S(2)}) copy-start(bf16[128,1,128]{0,2,1:T(8,128)(2,1)S(1)} %copy.26) | copy-start | bytes 98308
  23.0 3.7 %copy-start.20 = (bf16[128,1,128]{0,2,1:T(8,128)(2,1)}, bf16[128,1,128]{0,2,1:T(8,128)(2,1)S(1)}, u32[]{:S(2)}) copy-start(bf16[128,1,128]{0,2,1:T(8,128)(2,1)S(1)} %copy.28) | copy-start | bytes 98308
  35.4 9.6 %collective-permute-start.2 = (bf16[100,34,17]{0,1,2:T(8,128)(2,1)}, bf16[100,34,17]{0,1,2:T(8,128)(2,1)S(1)}, u32[]{:S(2)}, u32[]{:S(2)}) collective-permute-start(bf16[100,34,17]{0,1,2:T(8,128)(2,1)} %copy.31), channel_id=1, source_target_pairs={{0,1},{2,3},{4,5},{6,7},{8,9},{10,11},{12,13},{14,15},{16,17},{18,... | collective-permute-start | bytes 346808 | tf_op jit(solution)/shard_map/ppermute | solution.py:17
  41.3 7.5 %collective-permute-start.3 = (bf16[100,34,17]{0,1,2:T(8,128)(2,1)}, bf16[100,34,17]{0,1,2:T(8,128)(2,1)S(1)}, u32[]{:S(2)}, u32[]{:S(2)}) collective-permute-start(bf16[100,34,17]{0,1,2:T(8,128)(2,1)} %copy.34), channel_id=1, source_target_pairs={{1,0},{3,2},{5,4},{7,6},{9,8},{11,10},{13,12},{15,14},{17,16},{19,... | collective-permute-start | bytes 346808 | tf_op jit(solution)/shard_map/ppermute | solution.py:18
  44.9 9.1 %copy-start.14 = (bf16[100,34,17]{0,1,2:T(8,128)(2,1)}, bf16[100,34,17]{0,1,2:T(8,128)(2,1)S(1)}, u32[]{:S(2)}) copy-start(bf16[100,34,17]{0,1,2:T(8,128)(2,1)S(1)} %collective-permute-done.2) | copy-start | bytes 346804
  48.8 5.2 %copy-start.13 = (bf16[100,34,17]{0,1,2:T(8,128)(2,1)}, bf16[100,34,17]{0,1,2:T(8,128)(2,1)S(1)}, u32[]{:S(2)}) copy-start(bf16[100,34,17]{0,1,2:T(8,128)(2,1)S(1)} %collective-permute-done.3) | copy-start | bytes 346804
  54.0 0.9 %copy-start.24 = (pred[18,130]{1,0:T(8,128)(4,1)S(1)}, pred[18,130]{1,0:T(8,128)(4,1)}, u32[]{:S(2)}) copy-start(pred[18,130]{1,0:T(8,128)(4,1)} %broadcast_and_fusion) | copy-start | bytes 7024
  55.2 2.5 %copy-start.15 = (bf16[100,34,17]{0,1,2:T(8,128)(2,1)S(1)}, bf16[100,34,17]{0,1,2:T(8,128)(2,1)}, u32[]{:S(2)}) copy-start(bf16[100,34,17]{0,1,2:T(8,128)(2,1)} %copy-done.14) | copy-start | bytes 346804
  55.2 8.5 %copy-start.3 = (bf16[128,16,128]{0,2,1:T(8,128)(2,1)S(1)}, bf16[128,16,128]{0,2,1:T(8,128)(2,1)}, u32[]{:S(2)}) copy-start(bf16[128,16,128]{0,2,1:T(8,128)(2,1)} %copy-done.2) | copy-start | bytes 1572868
  55.2 8.5 %copy-start.19 = (bf16[128,1,128]{0,2,1:T(8,128)(2,1)S(1)}, bf16[128,1,128]{0,2,1:T(8,128)(2,1)}, u32[]{:S(2)}) copy-start(bf16[128,1,128]{0,2,1:T(8,128)(2,1)} %copy-done.18) | copy-start | bytes 98308
  55.2 8.5 %copy-start.21 = (bf16[128,1,128]{0,2,1:T(8,128)(2,1)S(1)}, bf16[128,1,128]{0,2,1:T(8,128)(2,1)}, u32[]{:S(2)}) copy-start(bf16[128,1,128]{0,2,1:T(8,128)(2,1)} %copy-done.20) | copy-start | bytes 98308
  64.4 1.0 %copy-start.17 = (bf16[3,3,128,224]{2,3,1,0:T(8,128)(2,1)S(1)}, bf16[3,3,128,224]{2,3,1,0:T(8,128)(2,1)}, u32[]{:S(2)}) copy-start(bf16[3,3,128,224]{2,3,1,0:T(8,128)(2,1)} %param.10) | copy-start | bytes 1548292
  64.4 1.3 %copy-start.11 = (bf16[96,16,128]{2,1,0:T(8,128)(2,1)S(1)}, bf16[96,16,128]{2,1,0:T(8,128)(2,1)}, u32[]{:S(2)}) copy-start(bf16[96,16,128]{2,1,0:T(8,128)(2,1)} %get-tuple-element.16) | copy-start | bytes 1179652
  65.4 1.1 %copy-start.5 = (bf16[128,16,128]{2,1,0:T(8,128)(2,1)S(1)}, bf16[128,16,128]{2,1,0:T(8,128)(2,1)}, u32[]{:S(2)}) copy-start(bf16[128,16,128]{2,1,0:T(8,128)(2,1)} %get-tuple-element.30) | copy-start | bytes 1572868
  65.7 1.1 %copy-start.10 = (bf16[96,16,128]{2,1,0:T(8,128)(2,1)S(1)}, bf16[96,16,128]{2,1,0:T(8,128)(2,1)}, u32[]{:S(2)}) copy-start(bf16[96,16,128]{2,1,0:T(8,128)(2,1)} %get-tuple-element.15) | copy-start | bytes 1179652
  66.8 1.0 %copy-start.9 = (bf16[96,16,128]{2,1,0:T(8,128)(2,1)S(1)}, bf16[96,16,128]{2,1,0:T(8,128)(2,1)}, u32[]{:S(2)}) copy-start(bf16[96,16,128]{2,1,0:T(8,128)(2,1)} %get-tuple-element.14) | copy-start | bytes 1179652
  67.8 1.0 %copy-start.8 = (bf16[96,16,128]{2,1,0:T(8,128)(2,1)S(1)}, bf16[96,16,128]{2,1,0:T(8,128)(2,1)}, u32[]{:S(2)}) copy-start(bf16[96,16,128]{2,1,0:T(8,128)(2,1)} %get-tuple-element.13) | copy-start | bytes 1179652
  68.8 1.0 %copy-start.7 = (bf16[96,16,128]{2,1,0:T(8,128)(2,1)S(1)}, bf16[96,16,128]{2,1,0:T(8,128)(2,1)}, u32[]{:S(2)}) copy-start(bf16[96,16,128]{2,1,0:T(8,128)(2,1)} %get-tuple-element.12) | copy-start | bytes 1179652
  69.8 1.0 %copy-start.6 = (bf16[96,16,128]{2,1,0:T(8,128)(2,1)S(1)}, bf16[96,16,128]{2,1,0:T(8,128)(2,1)}, u32[]{:S(2)}) copy-start(bf16[96,16,128]{2,1,0:T(8,128)(2,1)} %get-tuple-element.11) | copy-start | bytes 1179652
  71.2 1.0 %copy-start.4 = (bf16[128,16,128]{2,1,0:T(8,128)(2,1)S(1)}, bf16[128,16,128]{2,1,0:T(8,128)(2,1)}, u32[]{:S(2)}) copy-start(bf16[128,16,128]{2,1,0:T(8,128)(2,1)} %get-tuple-element.29) | copy-start | bytes 1572868
  72.6 1.0 %copy-start.12 = (bf16[96,16,128]{2,1,0:T(8,128)(2,1)S(1)}, bf16[96,16,128]{2,1,0:T(8,128)(2,1)}, u32[]{:S(2)}) copy-start(bf16[96,16,128]{2,1,0:T(8,128)(2,1)} %get-tuple-element.8) | copy-start | bytes 1179652
  72.6 1.0 %copy-start.26 = (f32[128]{0:T(128)S(1)}, f32[128]{0:T(128)}, u32[]{:S(2)}) copy-start(f32[128]{0:T(128)} %param.11) | copy-start | bytes 1540
where the time goes:
time: 76.3 us; the launch traced here: 75.1 us
  local copies, waits for them, and re-layouts  37.1 us (49%)
  starting transfers between devices  11.2 us (15%)
  other arithmetic  9.61 us (13%)
  between operations  8.16 us (11%)
  matrix products  6.75 us (9%)
  waiting for transfers between devices  2.27 us (3%)
    ppermute x2, starting transfers between devices, with_halo(): after = lax.ppermute(first, axis, down)  5.82 us
    ppermute x2, starting transfers between devices, with_halo(): before = lax.ppermute(last, axis, up)  5.33 us
    concatenate x2, other arithmetic, with_halo(): shard = jnp.concatenate([before, shard, after], axis=dim)  5.17 us
    unnamed x55, local copies, waits for them, and re-layouts  4.18 us
    slice x2, local copies, waits for them, and re-layouts, with_halo(): first = lax.slice_in_dim(shard, 0, width, axis=dim)  4.17 us
    another operation x3, local copies, waits for them, and re-layouts, body(): below_row[:, None, :]  3.68 us
    slice x2, local copies, waits for them, and re-layouts, with_halo(): last = lax.slice_in_dim(shard, length - width, length, axis=dim)  3.62 us
    dot_general x9, matrix products, conv_taps(): jnp.dot(mixer_weight[tap_row, tap_col, :, channels:], older, preferred_el...  3 us
  transfers between devices with their start and end apart: 4, of which 1 were waited for; matrix products, arithmetic and copies ran while one was open for 12% of the time, Pallas kernels for 0%

commit v1 on v0

v1 whole, which is shorter than its diff:
```python
import jax
import jax.numpy as jnp
from jax import lax
from jax.sharding import PartitionSpec as P

CP = 32
SHIFT_X = 16
SPLIT = True


def exchange(first, last, axis):
    size = lax.axis_size(axis)
    up = [(i, (i + 1) % size) for i in range(size - 1)]
    down = [(j, i) for i, j in up]
    return lax.ppermute(last, axis, up), lax.ppermute(first, axis, down)


def widen(block, rows, channels):
    return jnp.pad(block, ((0, rows - block.shape[0]), (0, 0), (0, channels - block.shape[2])))


def conv(block, weight):
    return lax.conv_general_dilated(
        block[None],
        weight,
        (1, 1),
        "VALID",
        dimension_numbers=("NHWC", "HWOI", "NHWC"),
        preferred_element_type=jnp.float32,
    )[0]


def body(current_frame, history_frames, offsets, compress_weight, mixer_weight, mixer_bias):
    frames, channels, height, width = history_frames.shape
    depth = frames * CP
    reach_rows = height // 2 + 1
    reach_cols = SHIFT_X + 1
    reduced = jnp.einsum(
        "oc,fcrx->rfox", compress_weight, history_frames, preferred_element_type=jnp.float32
    ).astype(jnp.bfloat16)
    source = reduced.reshape(height, depth, width).transpose(0, 2, 1)
    present = current_frame.transpose(1, 2, 0)
    wide = max(depth, channels)

    def row_pack(own, now):
        return jnp.concatenate([widen(own, reach_rows, wide), widen(now, 1, wide)], axis=0)

    above, below = exchange(
        row_pack(source[:reach_rows], present[:1]),
        row_pack(source[height - reach_rows :], present[height - 1 :]),
        "rows",
    )
    source = jnp.concatenate(
        [above[:reach_rows, :, :depth], source, below[:reach_rows, :, :depth]], axis=0
    )
    present = jnp.concatenate(
        [above[reach_rows:, :, :channels], present, below[reach_rows:, :, :channels]], axis=0
    )
    span = source.shape[0]

    def col_pack(own, now):
        return jnp.concatenate([widen(own, span, wide), widen(now, span, wide)], axis=1)

    left, right = exchange(
        col_pack(source[:, :reach_cols], present[:, :1]),
        col_pack(source[:, width - reach_cols :], present[:, width - 1 :]),
        "cols",
    )
    source = jnp.concatenate(
        [left[:, :reach_cols, :depth], source, right[:, :reach_cols, :depth]], axis=1
    )
    present = jnp.concatenate(
        [
            left[: height + 2, reach_cols:, :channels],
            present,
            right[: height + 2, reach_cols:, :channels],
        ],
        axis=1,
    )
    lane = lax.broadcasted_iota(jnp.int32, (1, 1, depth), 2) // CP
    shifted = None
    for k in range(frames):
        window = lax.dynamic_slice(
            source,
            (reach_rows - 1 - offsets[k, 0], reach_cols - 1 - offsets[k, 1], jnp.int32(0)),
            (height + 2, width + 2, depth),
        )
        shifted = window if shifted is None else jnp.where(lane == k, window, shifted)
    row = lax.broadcasted_iota(jnp.int32, (height + 2, 1, 1), 0) + (
        lax.axis_index("rows") * height - 1
    )
    col = lax.broadcasted_iota(jnp.int32, (1, width + 2, 1), 1) + (
        lax.axis_index("cols") * width - 1
    )
    inside = (row >= 0) & (row < height * lax.axis_size("rows"))
    inside = inside & (col >= 0) & (col < width * lax.axis_size("cols"))
    shifted = jnp.where(inside, shifted, jnp.zeros_like(shifted))
    if SPLIT:
        total = conv(present, mixer_weight[..., :channels])
        total = total + conv(shifted, mixer_weight[..., channels:])
    else:
        total = conv(jnp.concatenate([present, shifted], axis=2), mixer_weight)
    result = jnp.maximum(total + mixer_bias, 0.0).astype(jnp.bfloat16)
    return result.transpose(2, 0, 1)


def solution(mesh):
    in_specs = (P(None, "rows", "cols"), P(None, None, "rows", "cols"), P(), P(), P(), P())
    out_specs = P(None, "rows", "cols")
    return jax.shard_map(body, mesh=mesh, in_specs=in_specs, out_specs=out_specs, check_vma=False)
```

time: 76.3 us -> 66.7 us (0.87)
  the two profiles are of different devices: /device:TPU:8 before, /device:TPU:10 now
where the time goes in v1:
time: 66.7 us; the launch traced here: 65.9 us
  local copies, waits for them, and re-layouts  27.4 us (41%)
  starting transfers between devices  11 us (16%)
  waiting for transfers between devices  8.43 us (13%)
  between operations  7.68 us (12%)
  other arithmetic  7.57 us (11%)
  matrix products  3.76 us (6%)
    unnamed x43, local copies, waits for them, and re-layouts  12.3 us
    ppermute x4, starting transfers between devices, exchange(): return (lax.ppermute(last, axis, up), lax.ppermute(first, axis, down))  11 us
    ppermute x4, waiting for transfers between devices, exchange(): return (lax.ppermute(last, axis, up), lax.ppermute(first, axis, down))  8.43 us
    broadcast_in_dim x2, other arithmetic, conv(): block[None]  4.02 us
    conv_general_dilated x6, local copies, waits for them, and re-layouts, conv(): lax.conv_general_dilated(block[None], weight, (1, 1), 'VALID', dimension_...  3.57 us
    conv_general_dilated x2, matrix products, conv(): lax.conv_general_dilated(block[None], weight, (1, 1), 'VALID', dimension_...  2.7 us
    concatenate x1, other arithmetic, body(): jnp.concatenate([left[:, :reach_cols, :depth], source, right[:, :reach_co...  2.09 us
    broadcast_in_dim x2, local copies, waits for them, and re-layouts, conv(): block[None]  1.88 us
  transfers between devices with their start and end apart: 4, of which 2 were waited for; matrix products, arithmetic and copies ran while one was open for 2% of the time, Pallas kernels for 0%

profile of v1, /device:TPU:10, one launch (start us, length us, event | category | flops | bytes accessed | tf_op | source)
XLA Modules:
  0.0 65.9 jit_solution(17658822021721244742)
XLA Ops:
  0.0 1.4 %copy-done = bf16[3,128,16,128]{3,2,1,0:T(8,128)(2,1)S(1)} copy-done((bf16[3,128,16,128]{3,2,1,0:T(8,128)(2,1)S(1)}, bf16[3,128,16,128]{3,2,1,0:T(8,128)(2,1)}, u32[]{:S(2)}) %copy-start) | copy-done | bytes 1572888
  1.4 1.1 %fusion.8 = bf16[16,3,32,128]{3,2,0,1:T(8,128)(2,1)S(1)} fusion(bf16[3,128,16,128]{3,2,1,0:T(8,128)(2,1)S(1)} %copy-done, bf16[32,128]{1,0:T(8,128)(2,1)} %param.9), kind=kOutput, calls=%fused_computation.11 | convolution fusion | flops 50528256 | bytes 1974272 | tf_op jit(solution)/shard_map/oc,fcrx->rfox/dot_general | solution.py:38
  2.6 0.1 copy.58
  2.8 1.9 %collective-permute-start.1 = (bf16[10,128,128]{1,2,0:T(8,128)(2,1)S(1)}, bf16[10,128,128]{1,2,0:T(8,128)(2,1)S(1)}, u32[]{:S(2)}, u32[]{:S(2)}) collective-permute-start(bf16[10,128,128]{1,2,0:T(8,128)(2,1)S(1)} %fusion.36), channel_id=1, source_target_pairs={{2,0},{4,2},{6,4},{8,6},{10,8},{12,10},{14,12},{16,14},{18,16},{20... | collective-permute-start | bytes 983048 | tf_op jit(solution)/shard_map/ppermute | solution.py:15
  4.7 2.4 %collective-permute-start = (bf16[10,128,128]{1,2,0:T(8,128)(2,1)S(1)}, bf16[10,128,128]{1,2,0:T(8,128)(2,1)}, u32[]{:S(2)}, u32[]{:S(2)}) collective-permute-start(bf16[10,128,128]{1,2,0:T(8,128)(2,1)S(1)} %fusion.35), channel_id=1, source_target_pairs={{0,2},{2,4},{4,6},{6,8},{8,10},{10,12},{12,14},{14,16},{16,18},{18... | collective-permute-start | bytes 983048 | tf_op jit(solution)/shard_map/ppermute | solution.py:15
  7.2 0.1 and_and_fusion
  7.3 2.0 %collective-permute-done.1 = bf16[10,128,128]{1,2,0:T(8,128)(2,1)S(1)} collective-permute-done((bf16[10,128,128]{1,2,0:T(8,128)(2,1)S(1)}, bf16[10,128,128]{1,2,0:T(8,128)(2,1)S(1)}, u32[]{:S(2)}, u32[]{:S(2)}) %collective-permute-start.1) | collective-permute-done | bytes 327712 | tf_op jit(solution)/shard_map/ppermute | solution.py:15
  9.3 6.4 %collective-permute-done = bf16[10,128,128]{1,2,0:T(8,128)(2,1)} collective-permute-done((bf16[10,128,128]{1,2,0:T(8,128)(2,1)S(1)}, bf16[10,128,128]{1,2,0:T(8,128)(2,1)}, u32[]{:S(2)}, u32[]{:S(2)}) %collective-permute-start) | collective-permute-done | bytes 327712 | tf_op jit(solution)/shard_map/ppermute | solution.py:15
  15.7 0.8 %slice.106 = bf16[1,128,128]{1,2,0:T(8,128)(2,1)S(1)} slice(bf16[10,128,128]{1,2,0:T(8,128)(2,1)} %collective-permute-done), slice={[9:10], [0:128], [0:128]} | slice | bytes 65536 | tf_op jit(solution)/shard_map/slice | solution.py:57
  16.4 0.6 copy-done.8
  17.1 1.1 %fusion.51 = (bf16[18,1,128]{1,2,0:T(8,128)(2,1)}, bf16[18,1,128]{1,2,0:T(8,128)(2,1)S(1)}) fusion(bf16[18,128,128]{1,2,0:T(8,128)(2,1)S(1)} %pad_maximum_fusion.2), kind=kLoop, calls=%fused_computation.68 | loop fusion | bytes 18432 | tf_op jit(solution)/shard_map/slice | solution.py:66
  18.2 1.4 %copy.46 = bf16[18,1,128]{2,0,1:T(8,128)(2,1)S(1)} copy(bf16[18,1,128]{1,2,0:T(8,128)(2,1)} %get-tuple-element.7) | data formatting | bytes 9216
  19.6 0.9 %copy.48 = bf16[18,1,128]{2,0,1:T(8,128)(2,1)} copy(bf16[18,1,128]{1,2,0:T(8,128)(2,1)S(1)} %get-tuple-element.8) | data formatting | bytes 9216
  20.5 1.0 %slice.101 = bf16[9,128,96]{1,2,0:T(8,128)(2,1)S(1)} slice(bf16[10,128,128]{1,2,0:T(8,128)(2,1)} %collective-permute-done), slice={[0:9], [0:128], [0:96]} | slice | bytes 442368 | tf_op jit(solution)/shard_map/slice | solution.py:54
  21.6 0.7 %copy-done.3 = bf16[9,128,96]{1,2,0:T(8,128)(2,1)} copy-done((bf16[9,128,96]{1,2,0:T(8,128)(2,1)}, bf16[9,128,96]{1,2,0:T(8,128)(2,1)S(1)}, u32[]{:S(2)}) %copy-start.3) | copy-done | bytes 221208
  22.3 0.1 pad_maximum_fusion.1
  22.4 1.2 %fusion.50 = (bf16[34,17,96]{1,2,0:T(8,128)(2,1)}, bf16[34,17,96]{1,2,0:T(8,128)(2,1)S(1)}) fusion(bf16[34,128,96]{1,2,0:T(8,128)(2,1)S(1)} %pad_maximum_fusion.1), kind=kLoop, calls=%fused_computation.67 | loop fusion | bytes 443904 | tf_op jit(solution)/shard_map/slice | solution.py:66
  23.6 1.6 %copy.45 = bf16[34,17,96]{2,0,1:T(8,128)(2,1)S(1)} copy(bf16[34,17,96]{1,2,0:T(8,128)(2,1)} %get-tuple-element.5) | data formatting | bytes 221952
  25.2 1.1 %copy.47 = bf16[34,17,96]{2,0,1:T(8,128)(2,1)} copy(bf16[34,17,96]{1,2,0:T(8,128)(2,1)S(1)} %get-tuple-element.6) | data formatting | bytes 221952
  26.3 1.0 %fusion.40 = bf16[34,18,128]{2,0,1:T(8,128)(2,1)S(1)} fusion(bf16[18,1,128]{2,0,1:T(8,128)(2,1)} %copy.48, bf16[34,17,96]{2,0,1:T(8,128)(2,1)} %copy.47), kind=kLoop, calls=%fused_computation.48 | loop fusion | flops 626688 | bytes 272256 | tf_op jit(solution)/shard_map/concatenate | solution.py:62
  27.2 1.3 %collective-permute-start.3 = (bf16[34,18,128]{2,0,1:T(8,128)(2,1)S(1)}, bf16[34,18,128]{2,0,1:T(8,128)(2,1)}, u32[]{:S(2)}, u32[]{:S(2)}) collective-permute-start(bf16[34,18,128]{2,0,1:T(8,128)(2,1)S(1)} %fusion.40), channel_id=1, source_target_pairs={{1,0},{3,2},{5,4},{7,6},{9,8},{11,10},{13,12},{15,14},{17,16},{19,... | collective-permute-start | bytes 470024 | tf_op jit(solution)/shard_map/ppermute | solution.py:15
  28.6 5.4 %collective-permute-start.2 = (bf16[34,18,128]{2,0,1:T(8,128)(2,1)S(1)}, bf16[34,18,128]{2,0,1:T(8,128)(2,1)S(1)}, u32[]{:S(2)}, u32[]{:S(2)}) collective-permute-start(bf16[34,18,128]{2,0,1:T(8,128)(2,1)S(1)} %fusion.39), channel_id=1, source_target_pairs={{0,1},{2,3},{4,5},{6,7},{8,9},{10,11},{12,13},{14,15},{16,17},{18,... | collective-permute-start | bytes 470024 | tf_op jit(solution)/shard_map/ppermute | solution.py:15
  34.0 0.7 fusion.54
  42.0 0.4 copy.28
  42.4 0.7 %slice.112 = bf16[18,1,128]{2,0,1:T(8,128)(2,1)S(1)} slice(bf16[34,18,128]{2,0,1:T(8,128)(2,1)} %collective-permute-done.3), slice={[0:18], [17:18], [0:128]} | slice | bytes 9216 | tf_op jit(solution)/shard_map/slice | solution.py:76
  43.1 1.1 %copy.29 = bf16[18,1,128]{1,2,0:T(8,128)(2,1)} copy(bf16[18,1,128]{2,0,1:T(8,128)(2,1)S(1)} %slice.112) | data formatting | bytes 9216 | tf_op jit(solution)/shard_map/slice | solution.py:76
  44.2 2.8 %maximum_bitcast_fusion = bf16[18,1,130,128]{2,3,0,1:T(8,128)(2,1)} fusion(bf16[18,1,128]{1,2,0:T(8,128)(2,1)} %copy.29, bf16[1,128,128]{1,2,0:T(8,128)(2,1)S(1)} %slice.107, bf16[16,128,128]{1,2,0:T(8,128)(2,1)S(1)} %bitcast.61, bf16[1,128,128]{1,2,0:T(8,128)(2,1)S(1)} %copy-done.9, bf16[18,1,128]{1,2,0:T(8,128)(2,1)S(1)} %copy.28), kind=kLoop, calls=%fused_computation.12 | loop fusion | flops 2995200 | bytes 1198080 | tf_op jit(solution)/shard_map/broadcast_in_dim | solution.py:24
  47.0 1.7 %copy.49 = bf16[18,1,130,128]{3,2,0,1:T(8,128)(2,1)S(1)} copy(bf16[18,1,130,128]{2,3,0,1:T(8,128)(2,1)} %maximum_bitcast_fusion) | data formatting | bytes 1198080
  48.6 0.9 %pad.27.clone = bf16[18,1,136,128]{3,2,0,1:T(8,128)(2,1)} pad(bf16[18,1,130,128]{3,2,0,1:T(8,128)(2,1)S(1)} %copy.49, bf16[]{:T(256)} %constant.57.clone.1), padding=0_0x0_0x0_6x0_0 | pad | bytes 1225730 | tf_op jit(solution)/shard_map/broadcast_in_dim | solution.py:24
  49.5 1.3 %reshape.143 = bf16[18,1,8,17,128]{4,3,2,0,1:T(8,128)(2,1)S(1)} reshape(bf16[18,1,136,128]{3,2,0,1:T(8,128)(2,1)} %pad.27.clone) | data formatting | bytes 1253376 | tf_op jit(solution)/shard_map/conv_general_dilated | solution.py:23
  50.9 0.1 copy.32
  51.0 0.7 slice.113
  51.6 0.2 copy-done.5
  51.8 0.4 copy.43
  52.3 0.9 %slice.115 = bf16[34,17,96]{2,0,1:T(8,128)(2,1)S(1)} slice(bf16[34,18,128]{2,0,1:T(8,128)(2,1)} %collective-permute-done.3), slice={[0:34], [0:17], [0:96]} | slice | bytes 221952 | tf_op jit(solution)/shard_map/slice | solution.py:70
  53.2 1.3 %copy.44 = bf16[34,17,96]{1,2,0:T(8,128)(2,1)} copy(bf16[34,17,96]{2,0,1:T(8,128)(2,1)S(1)} %slice.115) | data formatting | bytes 221952
  54.6 2.1 %pad_maximum_fusion = bf16[34,162,96]{1,2,0:T(8,128)(2,1)S(1)} fusion(bf16[34,17,96]{1,2,0:T(8,128)(2,1)} %copy.44, bf16[9,128,96]{1,2,0:T(8,128)(2,1)S(1)} %copy-done.2, bf16[16,128,96]{1,2,0:T(8,128)(2,1)S(1)} %bitcast.58, bf16[9,128,96]{1,2,0:T(8,128)(2,1)S(1)} %copy-done.4, bf16[34,17,96]{1,2,0:T(8,128)(2,1)S(1)} %copy.43), kind=kLoop, calls=%fused_computation | loop fusion | flops 5287680 | bytes 2115072 | tf_op jit(solution)/shard_map/concatenate | solution.py:69
  56.6 1.2 %select_bitcast_fusion = bf16[18,1,130,96]{2,3,0,1:T(8,128)(2,1)S(1)} fusion(bf16[34,162,96]{1,2,0:T(8,128)(2,1)S(1)} %pad_maximum_fusion, s32[]{:T(128)S(6)} %select_n.49, s32[]{:T(128)S(6)} %select_n.50, s32[]{:T(128)S(6)} %select_n.47, s32[]{:T(128)S(6)} %select_n.48, s32[]{:T(128)S(6)} %select_n.45, s32[]{:T(128)S(6)} %select_n.46, ...), kind=kLoop, calls=%fused_computation.17 | loop fusion | flops 673920 | bytes 1799676 | tf_op jit(solution)/shard_map/broadcast_in_dim | solution.py:24
  57.9 0.4 copy.50
  58.3 1.0 %pad.29.clone = bf16[18,1,136,96]{3,2,0,1:T(8,128)(2,1)} pad(bf16[18,1,130,96]{3,2,0,1:T(8,128)(2,1)S(1)} %copy.50, bf16[]{:T(256)} %constant.57.clone.1), padding=0_0x0_0x0_6x0_0 | pad | bytes 919298 | tf_op jit(solution)/shard_map/broadcast_in_dim | solution.py:24
  59.3 1.4 %reshape.148 = bf16[18,1,8,17,96]{4,3,2,0,1:T(8,128)(2,1)S(1)} reshape(bf16[18,1,136,96]{3,2,0,1:T(8,128)(2,1)} %pad.29.clone) | data formatting | bytes 940032 | tf_op jit(solution)/shard_map/conv_general_dilated | solution.py:23
  60.7 0.1 copy.38
  60.9 1.2 %convolution_select_fusion = f32[16,8,17,128]{3,1,2,0:T(8,128)S(1)} fusion(bf16[18,1,7,2,96]{4,2,3,0,1:T(8,128)(2,1)S(1)} %slice.116, bf16[18,1,8,17,96]{4,2,3,0,1:T(8,128)(2,1)S(1)} %copy.38, pred[8,17]{0,1:T(8,128)(4,1)S(1)} %copy-done.16, bf16[3,3,128,224]{2,3,1,0:T(8,128)(2,1)S(1)} %copy-done.15), kind=kOutput, calls=%fused_computation.7 | convolution fusion | flops 483150848 | bytes 2038784 | tf_op jit(solution)/shard_map/conv_general_dilated | solution.py:23
  62.1 1.5 %fusion.4 = f32[16,8,17,128]{3,1,2,0:T(8,128)S(1)} fusion(f32[16,8,17,128]{3,1,2,0:T(8,128)S(1)} %convolution_select_fusion, bf16[18,1,7,2,128]{4,2,3,0,1:T(8,128)(2,1)S(1)} %copy-done.12, bf16[18,1,8,17,128]{4,2,3,0,1:T(8,128)(2,1)S(1)} %copy-done.6, pred[8,17]{0,1:T(8,128)(4,1)S(1)} %copy-done.16, bf16[3,3,128,224]{2,3,1,0:T(8,128)(2,1)S(1)} %copy-done.15), kind=kOutput, calls=%fused_computation.9 | convolution fusion | flops 644386816 | bytes 3226624 | tf_op jit(solution)/shard_map/conv_general_dilated | solution.py:23
  63.6 0.2 copy.39
  63.9 0.4 copy-done.14
  64.3 0.1 fusion.28
  64.4 1.5 %copy.40 = bf16[128,16,128]{2,1,0:T(8,128)(2,1)} copy(bf16[128,16,128]{0,1,2:T(8,128)(2,1)S(1)} %fusion.28) | data formatting | bytes 1048576 | tf_op jit(solution)/shard_map/transpose | solution.py:104
  (46 shorter events, 0.4 us)
Async XLA Ops:
  0.0 1.4 %copy-start = (bf16[3,128,16,128]{3,2,1,0:T(8,128)(2,1)S(1)}, bf16[3,128,16,128]{3,2,1,0:T(8,128)(2,1)}, u32[]{:S(2)}) copy-start(bf16[3,128,16,128]{3,2,1,0:T(8,128)(2,1)} %param.7) | copy-start | bytes 4718596
  0.0 2.6 %copy-start.7 = (bf16[128,16,128]{2,1,0:T(8,128)(2,1)S(1)}, bf16[128,16,128]{2,1,0:T(8,128)(2,1)}, u32[]{:S(2)}) copy-start(bf16[128,16,128]{2,1,0:T(8,128)(2,1)} %param.6) | copy-start | bytes 1572868
  2.8 6.5 %collective-permute-start.1 = (bf16[10,128,128]{1,2,0:T(8,128)(2,1)S(1)}, bf16[10,128,128]{1,2,0:T(8,128)(2,1)S(1)}, u32[]{:S(2)}, u32[]{:S(2)}) collective-permute-start(bf16[10,128,128]{1,2,0:T(8,128)(2,1)S(1)} %fusion.36), channel_id=1, source_target_pairs={{2,0},{4,2},{6,4},{8,6},{10,8},{12,10},{14,12},{16,14},{18,16},{20... | collective-permute-start | bytes 983048 | tf_op jit(solution)/shard_map/ppermute | solution.py:15
  4.7 11.0 %collective-permute-start = (bf16[10,128,128]{1,2,0:T(8,128)(2,1)S(1)}, bf16[10,128,128]{1,2,0:T(8,128)(2,1)}, u32[]{:S(2)}, u32[]{:S(2)}) collective-permute-start(bf16[10,128,128]{1,2,0:T(8,128)(2,1)S(1)} %fusion.35), channel_id=1, source_target_pairs={{0,2},{2,4},{4,6},{6,8},{8,10},{10,12},{12,14},{14,16},{16,18},{18... | collective-permute-start | bytes 983048 | tf_op jit(solution)/shard_map/ppermute | solution.py:15
  16.4 0.6 copy-start.8
  20.5 1.1 %copy-start.1 = (bf16[9,128,96]{1,2,0:T(8,128)(2,1)}, bf16[9,128,96]{1,2,0:T(8,128)(2,1)S(1)}, u32[]{:S(2)}) copy-start(bf16[9,128,96]{1,2,0:T(8,128)(2,1)S(1)} %slice.104) | copy-start | bytes 663556
  21.6 0.7 %copy-start.3 = (bf16[9,128,96]{1,2,0:T(8,128)(2,1)}, bf16[9,128,96]{1,2,0:T(8,128)(2,1)S(1)}, u32[]{:S(2)}) copy-start(bf16[9,128,96]{1,2,0:T(8,128)(2,1)S(1)} %slice.101) | copy-start | bytes 663556
  23.6 10.4 %copy-start.13 = (s32[3,2]{0,1:T(2,128)S(1)}, s32[3,2]{0,1:T(2,128)}, u32[]{:S(2)}) copy-start(s32[3,2]{0,1:T(2,128)} %param.8) | copy-start | bytes 76
  26.3 17.9 %copy-start.9 = (bf16[1,128,128]{1,2,0:T(8,128)(2,1)S(1)}, bf16[1,128,128]{1,2,0:T(8,128)(2,1)}, u32[]{:S(2)}) copy-start(bf16[1,128,128]{1,2,0:T(8,128)(2,1)} %copy-done.8) | copy-start | bytes 98308
  27.2 15.1 %collective-permute-start.3 = (bf16[34,18,128]{2,0,1:T(8,128)(2,1)S(1)}, bf16[34,18,128]{2,0,1:T(8,128)(2,1)}, u32[]{:S(2)}, u32[]{:S(2)}) collective-permute-start(bf16[34,18,128]{2,0,1:T(8,128)(2,1)S(1)} %fusion.40), channel_id=1, source_target_pairs={{1,0},{3,2},{5,4},{7,6},{9,8},{11,10},{13,12},{15,14},{17,16},{19,... | collective-permute-start | bytes 470024 | tf_op jit(solution)/shard_map/ppermute | solution.py:15
  28.6 13.4 %collective-permute-start.2 = (bf16[34,18,128]{2,0,1:T(8,128)(2,1)S(1)}, bf16[34,18,128]{2,0,1:T(8,128)(2,1)S(1)}, u32[]{:S(2)}, u32[]{:S(2)}) collective-permute-start(bf16[34,18,128]{2,0,1:T(8,128)(2,1)S(1)} %fusion.39), channel_id=1, source_target_pairs={{0,1},{2,3},{4,5},{6,7},{8,9},{10,11},{12,13},{14,15},{16,17},{18,... | collective-permute-start | bytes 470024 | tf_op jit(solution)/shard_map/ppermute | solution.py:15
  42.0 5.0 %copy-start.10 = (bf16[34,18,128]{2,0,1:T(8,128)(2,1)}, bf16[34,18,128]{2,0,1:T(8,128)(2,1)S(1)}, u32[]{:S(2)}) copy-start(bf16[34,18,128]{2,0,1:T(8,128)(2,1)S(1)} %collective-permute-done.2) | copy-start | bytes 470020
  50.8 1.0 %copy-start.11 = (bf16[34,18,128]{2,0,1:T(8,128)(2,1)S(1)}, bf16[34,18,128]{2,0,1:T(8,128)(2,1)}, u32[]{:S(2)}) copy-start(bf16[34,18,128]{2,0,1:T(8,128)(2,1)} %copy-done.10) | copy-start | bytes 470020
  50.9 0.9 %copy-start.5 = (bf16[18,1,8,17,128]{4,2,3,0,1:T(8,128)(2,1)}, bf16[18,1,8,17,128]{4,2,3,0,1:T(8,128)(2,1)S(1)}, u32[]{:S(2)}) copy-start(bf16[18,1,8,17,128]{4,2,3,0,1:T(8,128)(2,1)S(1)} %copy.32) | copy-start | bytes 1880068
  51.0 3.6 %copy-start.2 = (bf16[9,128,96]{1,2,0:T(8,128)(2,1)S(1)}, bf16[9,128,96]{1,2,0:T(8,128)(2,1)}, u32[]{:S(2)}) copy-start(bf16[9,128,96]{1,2,0:T(8,128)(2,1)} %copy-done.1) | copy-start | bytes 663556
  51.0 3.6 %copy-start.4 = (bf16[9,128,96]{1,2,0:T(8,128)(2,1)S(1)}, bf16[9,128,96]{1,2,0:T(8,128)(2,1)}, u32[]{:S(2)}) copy-start(bf16[9,128,96]{1,2,0:T(8,128)(2,1)} %copy-done.3) | copy-start | bytes 663556
  59.3 1.6 %copy-start.15 = (bf16[3,3,128,224]{2,3,1,0:T(8,128)(2,1)S(1)}, bf16[3,3,128,224]{2,3,1,0:T(8,128)(2,1)}, u32[]{:S(2)}) copy-start(bf16[3,3,128,224]{2,3,1,0:T(8,128)(2,1)} %param.10) | copy-start | bytes 1548292
  59.3 1.6 %copy-start.16 = (pred[8,17]{0,1:T(8,128)(4,1)S(1)}, pred[8,17]{0,1:T(8,128)(4,1)}, u32[]{:S(2)}) copy-start(pred[8,17]{0,1:T(8,128)(4,1)} %constant.94) | copy-start | bytes 412
  60.9 1.3 %copy-start.6 = (bf16[18,1,8,17,128]{4,2,3,0,1:T(8,128)(2,1)S(1)}, bf16[18,1,8,17,128]{4,2,3,0,1:T(8,128)(2,1)}, u32[]{:S(2)}) copy-start(bf16[18,1,8,17,128]{4,2,3,0,1:T(8,128)(2,1)} %copy-done.5) | copy-start | bytes 1880068
  60.9 1.3 %copy-start.12 = (bf16[18,1,7,2,128]{4,2,3,0,1:T(8,128)(2,1)S(1)}, bf16[18,1,7,2,128]{4,2,3,0,1:T(8,128)(2,1)}, u32[]{:S(2)}) copy-start(bf16[18,1,7,2,128]{4,2,3,0,1:T(8,128)(2,1)} %slice.113) | copy-start | bytes 193540
  63.6 0.7 copy-start.14
